TPU v7x, 32 devices: a whole 2x2x4 slice. The times are simulated.
32 devices in a mesh: row: 4 (over y, x), col: 4 (over z), crop: 2 (over core).
Axes of the slice: x: 2, y: 2, z: 4, core: 2. Of those that a mesh axis runs over, the one named last changes fastest.
Arguments:
- pair_repr: bfloat16 [256, 128, 128], P(('crop', 'row'), 'col'), parts along dimension 0, may hold values from -6 to 6
- pair_mask: int32 [256, 128], P(('crop', 'row'), 'col'), parts along dimension 0, may hold values 0 or 1
- out_left_w: bfloat16 [128, 256], replicated, may hold values from -0.5 to 0.5
- out_right_w: bfloat16 [128, 256], replicated, may hold values from -0.5 to 0.5
- out_gate_w: bfloat16 [128, 128], replicated, may hold values from -0.5 to 0.5
- out_final_w: bfloat16 [128, 128], replicated, may hold values from -0.5 to 0.5
- in_left_w: bfloat16 [128, 256], replicated, may hold values from -0.5 to 0.5
- in_right_w: bfloat16 [128, 256], replicated, may hold values from -0.5 to 0.5
- in_gate_w: bfloat16 [128, 128], replicated, may hold values from -0.5 to 0.5
- in_final_w: bfloat16 [128, 128], replicated, may hold values from -0.5 to 0.5
- trans_in_w: bfloat16 [128, 1024], replicated, may hold values from -0.5 to 0.5
- trans_out_w: bfloat16 [512, 128], replicated, may hold values from -0.25 to 0.25
Outputs:
- pair_out: bfloat16 [256, 128, 128], P(('crop', 'row'), 'col'), parts along dimension 0
There are 2 independent parts, one for each index of `crop`. A program takes and returns all parts, laid end to end along the dimension named above; an argument that names none is the same for every part. Nothing has to cross between parts.
All inputs are finite; a program needn't handle non-finite values. No bound on the sum of `pair_mask` on one device may be relied on, other than what follows from the above.
Results may differ from a plain program's by a relative error of at most 0.015.
Values may be sent and summed in bfloat16 or wider, within the bound.
No kernel may reach another device: no remote copies, remote signals or barrier semaphores. Data moves between devices by JAX's collectives and lax.ppermute only.
A program may use at most 128 MiB of HBM per device.

v0:
```python
import jax
import jax.numpy as jnp
from jax import lax
from jax.sharding import PartitionSpec as P

epsilon = 1e-05


def layer_norm(values):
    average = jnp.mean(values, axis=-1, keepdims=True)
    centered = values - average
    spread = jnp.mean(centered * centered, axis=-1, keepdims=True)
    return centered * lax.rsqrt(spread + epsilon)


def gated(normed, weight, mask_vals):
    projected = jnp.dot(normed, weight, preferred_element_type=jnp.float32)
    half_width = weight.shape[1] // 2
    result = jax.nn.sigmoid(projected[..., :half_width]) * projected[..., half_width:]
    result = result * mask_vals[..., None]
    return result.astype(jnp.bfloat16)


def finish(pair_repr, normed, triangle, gate_w, final_w):
    gate_vals = jax.nn.sigmoid(jnp.dot(normed, gate_w, preferred_element_type=jnp.float32))
    tri_norm = layer_norm(triangle).astype(jnp.bfloat16)
    update = jnp.dot(tri_norm, final_w, preferred_element_type=jnp.float32)
    return (pair_repr.astype(jnp.float32) + gate_vals * update).astype(jnp.bfloat16)


def shards(
    pair_repr,
    pair_mask,
    out_left_w,
    out_right_w,
    out_gate_w,
    out_final_w,
    in_left_w,
    in_right_w,
    in_gate_w,
    in_final_w,
    trans_in_w,
    trans_out_w,
):
    mask_vals = pair_mask.astype(jnp.float32)
    normed_out = layer_norm(pair_repr.astype(jnp.float32)).astype(jnp.bfloat16)
    outbound = gated(normed_out, out_right_w, mask_vals)
    turned_right = lax.all_to_all(
        lax.all_to_all(outbound, "row", split_axis=0, concat_axis=0, tiled=True),
        "col",
        split_axis=0,
        concat_axis=1,
        tiled=True,
    )
    left_tile = gated(normed_out, out_left_w, mask_vals)
    gathered = lax.all_gather(left_tile, "col", axis=1, tiled=True)
    triangle = jnp.einsum(
        "ikh,jkh->ijh",
        gathered,
        lax.all_gather(turned_right, "row", axis=0, tiled=True),
        preferred_element_type=jnp.float32,
    )
    middle = finish(pair_repr, normed_out, triangle, out_gate_w, out_final_w)
    normed_in = layer_norm(middle.astype(jnp.float32)).astype(jnp.bfloat16)
    outbound_left = gated(normed_in, in_left_w, mask_vals)
    turned_left = lax.all_to_all(
        lax.all_to_all(outbound_left, "col", split_axis=1, concat_axis=1, tiled=True),
        "row",
        split_axis=1,
        concat_axis=0,
        tiled=True,
    )
    right_tile = gated(normed_in, in_right_w, mask_vals)
    column_panel = lax.all_gather(right_tile, "row", axis=0, tiled=True)
    triangle_in = jnp.einsum(
        "kih,kjh->ijh",
        lax.all_gather(turned_left, "col", axis=1, tiled=True),
        column_panel,
        preferred_element_type=jnp.float32,
    )
    after_in = finish(middle, normed_in, triangle_in, in_gate_w, in_final_w)
    normed_mix = layer_norm(after_in.astype(jnp.float32)).astype(jnp.bfloat16)
    projected = jnp.dot(normed_mix, trans_in_w, preferred_element_type=jnp.float32)
    half_width = trans_in_w.shape[1] // 2
    hidden = (jax.nn.silu(projected[..., :half_width]) * projected[..., half_width:]).astype(
        jnp.bfloat16
    )
    result = after_in.astype(jnp.float32) + jnp.dot(
        hidden, trans_out_w, preferred_element_type=jnp.float32
    )
    return result.astype(jnp.bfloat16)


def solution(mesh):
    in_specs = (
        P(("crop", "row"), "col", None),
        P(("crop", "row"), "col"),
        P(),
        P(),
        P(),
        P(),
        P(),
        P(),
        P(),
        P(),
        P(),
        P(),
    )
    out_specs = P(("crop", "row"), "col", None)
    return jax.shard_map(shards, mesh=mesh, in_specs=in_specs, out_specs=out_specs, check_vma=False)
```

profile of v0, /device:TPU:0, one launch (start us, length us, event | category | flops | bytes accessed | tf_op | source)
XLA Modules:
  0.0 162.0 jit_solution(13725264176336256992)
XLA Ops:
  6.5 1.2 convert_reduce_fusion
  7.8 1.3 fusion.17
  9.1 1.4 fusion.44
  10.6 1.3 fusion.46
  13.0 10.7 %all_to_all.46 = bf16[32,32,128]{2,1,0:T(8,128)(2,1)S(1)} all-to-all(bf16[32,32,128]{2,1,0:T(8,128)(2,1)S(1)} %get-tuple-element.8), channel_id=1, replica_groups=mesh['row'=4,'col'=4,'crop'=2] {'row'}, dimensions={0} | all-to-all | bytes 524288 | tf_op jit(solution)/shard_map/all_to_all | solution.py:49
  23.7 21.0 %all_to_all.47 = bf16[32,32,128]{2,1,0:T(8,128)(2,1)S(1)} all-to-all(bf16[32,32,128]{2,1,0:T(8,128)(2,1)S(1)} %all_to_all.46), channel_id=1, replica_groups=mesh['row'=4,'col'=4,'crop'=2] {'col'}, dimensions={0} | all-to-all | bytes 524288 | tf_op jit(solution)/shard_map/all_to_all | solution.py:48
  46.5 3.4 %all-gather.7.cloned.1.call-done = bf16[32,128,128]{2,1,0:T(8,128)(2,1)} async-done(((bf16[32,32,128]{2,1,0:T(8,128)(2,1)}), bf16[32,128,128]{2,1,0:T(8,128)(2,1)}) %all-gather.7.cloned.1.call-update) | async-done | bytes 1048592 | tf_op jit(solution)/shard_map/all_gather | solution.py:56
  49.9 2.7 %copy.67 = bf16[32,128,128]{1,0,2:T(8,128)(2,1)} copy(bf16[32,128,128]{2,1,0:T(8,128)(2,1)} %all-gather.7.cloned.1.call-done) | data formatting | bytes 2097152 | tf_op jit(solution)/shard_map/all_gather | solution.py:56
  52.5 24.4 %all-gather.5.cloned.1.call-done = bf16[32,128,128]{1,0,2:T(8,128)(2,1)} async-done(((bf16[8,128,128]{1,0,2:T(8,128)(2,1)}), bf16[32,128,128]{1,0,2:T(8,128)(2,1)}) %all-gather.5.cloned.1.call-update) | async-done | bytes 1048592 | tf_op jit(solution)/shard_map/all_gather | solution.py:60
  76.9 2.2 %bitcast_reduce_fusion.1 = (f32[32,32]{0,1:T(8,128)S(1)}, f32[128,32,32]{2,1,0:T(8,128)S(1)}) fusion(bf16[32,128,128]{1,0,2:T(8,128)(2,1)} %all-gather.5.cloned.1.call-done, bf16[32,128,128]{1,0,2:T(8,128)(2,1)} %copy.67), kind=kOutput, calls=%fused_computation.5 | convolution fusion | flops 33684480 | bytes 2625536 | tf_op jit(solution)/shard_map/ikh,jkh->ijh/dot_general | solution.py:57
  79.8 1.3 multiply_convert_fusion.1
  81.1 2.7 %copy.72 = bf16[32,32,128]{2,1,0:T(8,128)(2,1)S(1)} copy(bf16[32,32,128]{0,1,2:T(8,128)(2,1)} %multiply_convert_fusion.1) | data formatting | bytes 524288 | tf_op jit(solution)/shard_map/convert_element_type | solution.py:26
  85.5 1.0 fusion.20
  86.7 13.1 %all_to_all.48 = bf16[32,32,128]{2,0,1:T(8,128)(2,1)S(1)} all-to-all(bf16[32,32,128]{2,0,1:T(8,128)(2,1)S(1)} %copy.73), channel_id=1, replica_groups=mesh['row'=4,'col'=4,'crop'=2] {'col'}, dimensions={1} | all-to-all | bytes 524288 | tf_op jit(solution)/shard_map/all_to_all | solution.py:67
  99.8 8.2 %all_to_all.49 = bf16[32,32,128]{2,0,1:T(8,128)(2,1)S(1)} all-to-all(bf16[32,32,128]{2,0,1:T(8,128)(2,1)S(1)} %all_to_all.48), channel_id=1, replica_groups=mesh['row'=4,'col'=4,'crop'=2] {'row'}, dimensions={1} | all-to-all | bytes 524288 | tf_op jit(solution)/shard_map/all_to_all | solution.py:66
  109.1 1.1 fusion.3
  110.2 3.4 %all-gather.9.cloned.1.call-done = bf16[128,32,128]{2,1,0:T(8,128)(2,1)} async-done(((bf16[32,32,128]{2,1,0:T(8,128)(2,1)}), bf16[128,32,128]{2,1,0:T(8,128)(2,1)}) %all-gather.9.cloned.1.call-update) | async-done | bytes 1048592 | tf_op jit(solution)/shard_map/all_gather | solution.py:74
  113.6 3.2 %copy.77 = bf16[128,32,128]{0,1,2:T(8,128)(2,1)} copy(bf16[128,32,128]{2,1,0:T(8,128)(2,1)} %all-gather.9.cloned.1.call-done) | data formatting | bytes 2097152 | tf_op jit(solution)/shard_map/all_gather | solution.py:74
  116.8 27.7 %all-gather.11.cloned.1.call-done = bf16[128,32,128]{0,1,2:T(8,128)(2,1)} async-done(((bf16[128,8,128]{0,1,2:T(8,128)(2,1)}), bf16[128,32,128]{0,1,2:T(8,128)(2,1)}) %all-gather.11.cloned.1.call-update) | async-done | bytes 1048592 | tf_op jit(solution)/shard_map/all_gather | solution.py:77
  144.5 2.2 %bitcast_reduce_fusion = (f32[32,32]{0,1:T(8,128)S(1)}, f32[128,32,32]{2,1,0:T(8,128)S(1)}) fusion(bf16[128,32,128]{0,1,2:T(8,128)(2,1)} %copy.77, bf16[128,32,128]{0,1,2:T(8,128)(2,1)} %all-gather.11.cloned.1.call-done), kind=kOutput, calls=%fused_computation.3 | convolution fusion | flops 33684480 | bytes 2625536 | tf_op jit(solution)/shard_map/kih,kjh->ijh/dot_general | solution.py:75
  147.4 1.3 multiply_convert_fusion
  148.6 2.6 %copy.82 = bf16[32,32,128]{2,1,0:T(8,128)(2,1)S(1)} copy(bf16[32,32,128]{0,1,2:T(8,128)(2,1)} %multiply_convert_fusion) | data formatting | bytes 524288 | tf_op jit(solution)/shard_map/convert_element_type | solution.py:26
  151.3 1.4 fusion.61
  154.0 1.4 fusion.13
  (63 shorter events, 8.2 us)
Async XLA Ops:
  6.5 146.6 %copy-start = (bf16[128,1024]{1,0:T(8,128)(2,1)S(1)}, bf16[128,1024]{1,0:T(8,128)(2,1)}, u32[]{:S(2)}) copy-start(bf16[128,1024]{1,0:T(8,128)(2,1)} %param.22) | copy-start | bytes 786436
  6.5 4.0 %copy-start.1 = (bf16[32,32,128]{2,1,0:T(8,128)(2,1)S(1)}, bf16[32,32,128]{2,1,0:T(8,128)(2,1)}, u32[]{:S(2)}) copy-start(bf16[32,32,128]{2,1,0:T(8,128)(2,1)} %param.12) | copy-start | bytes 786436
  6.5 5.3 %copy-start.6 = (s32[32,32]{1,0:T(8,128)S(1)}, s32[32,32]{1,0:T(8,128)}, u32[]{:S(2)}) copy-start(s32[32,32]{1,0:T(8,128)} %param.13) | copy-start | bytes 12292
  6.5 43.3 %all-gather.7.cloned.1.call-start = ((), (), s32[]{:S(2)}) async-start(), calls=%async_computation.5 | async-start | bytes 1310720 | tf_op jit(solution)/shard_map/all_gather | solution.py:56
  11.9 33.8 %copy-start.8 = (bf16[128,128]{1,0:T(8,128)(2,1)S(1)}, bf16[128,128]{1,0:T(8,128)(2,1)}, u32[]{:S(2)}) copy-start(bf16[128,128]{1,0:T(8,128)(2,1)} %param.16) | copy-start | bytes 98308
  12.9 64.0 %all-gather.5.cloned.1.call-start = ((), (), s32[]{:S(2)}) async-start(), calls=%async_computation.4 | async-start | bytes 1310720 | tf_op jit(solution)/shard_map/all_gather | solution.py:60
  45.7 67.9 %all-gather.9.cloned.1.call-start = ((), (), s32[]{:S(2)}) async-start(), calls=%async_computation.6 | async-start | bytes 1310720 | tf_op jit(solution)/shard_map/all_gather | solution.py:74
  79.8 3.9 %copy-start.5 = (bf16[128,128]{1,0:T(8,128)(2,1)S(1)}, bf16[128,128]{1,0:T(8,128)(2,1)}, u32[]{:S(2)}) copy-start(bf16[128,128]{1,0:T(8,128)(2,1)} %param.17) | copy-start | bytes 98308
  81.1 3.8 %copy-start.2 = (bf16[128,256]{1,0:T(8,128)(2,1)S(1)}, bf16[128,256]{1,0:T(8,128)(2,1)}, u32[]{:S(2)}) copy-start(bf16[128,256]{1,0:T(8,128)(2,1)} %param.18) | copy-start | bytes 196612
  83.7 1.4 copy-start.3
  86.5 22.6 %copy-start.9 = (bf16[128,128]{1,0:T(8,128)(2,1)S(1)}, bf16[128,128]{1,0:T(8,128)(2,1)}, u32[]{:S(2)}) copy-start(bf16[128,128]{1,0:T(8,128)(2,1)} %param.20) | copy-start | bytes 98308
  86.5 58.0 %all-gather.11.cloned.1.call-start = ((), (), s32[]{:S(2)}) async-start(), calls=%async_computation.7 | async-start | bytes 1310720 | tf_op jit(solution)/shard_map/all_gather | solution.py:77
  147.4 3.9 %copy-start.4 = (bf16[128,128]{1,0:T(8,128)(2,1)S(1)}, bf16[128,128]{1,0:T(8,128)(2,1)}, u32[]{:S(2)}) copy-start(bf16[128,128]{1,0:T(8,128)(2,1)} %param.21) | copy-start | bytes 98308
  153.1 0.9 copy-start.7
Sparse Core Ops, SparseCore 0:
  13.1 36.7 all-gather.6
  51.7 25.2 all-gather.4
  86.6 26.9 all-gather.8
  115.0 29.4 all-gather.10
where the time goes:
time: 163 us; the launch traced here: 162 us
  waiting for transfers between devices  59 us (36%)
  blocking collectives  53.1 us (33%)
  local copies, waits for them, and re-layouts  14 us (9%)
  matrix products  13.4 us (8%)
  between operations  13.4 us (8%)
  other arithmetic  8.94 us (5%)
    all_gather x1, waiting for transfers between devices, shards(): lax.all_gather(turned_left, 'col', axis=1, tiled=True)  27.7 us
    all_gather x1, waiting for transfers between devices, shards(): lax.all_gather(turned_right, 'row', axis=0, tiled=True)  24.4 us
    all_to_all x1, blocking collectives, shards(): lax.all_to_all(lax.all_to_all(outbound, 'row', split_axis=0, concat_axis=...  21 us
    all_to_all x1, blocking collectives, shards(): lax.all_to_all(outbound_left, 'col', split_axis=1, concat_axis=1, tiled=T...  13.1 us
    all_to_all x1, blocking collectives, shards(): lax.all_to_all(outbound, 'row', split_axis=0, concat_axis=0, tiled=True)  10.7 us
    all_to_all x1, blocking collectives, shards(): lax.all_to_all(lax.all_to_all(outbound_left, 'col', split_axis=1, concat_...  8.25 us
    convert_element_type x2, local copies, waits for them, and re-layouts, finish(): tri_norm = layer_norm(triangle).astype(jnp.bfloat16)  5.27 us
    all_gather x1, waiting for transfers between devices, shards(): column_panel = lax.all_gather(right_tile, 'row', axis=0, tiled=True)  3.41 us
  transfers between devices with their start and end apart: 4, of which 4 were waited for; matrix products, arithmetic and copies ran while one was open for 6% of the time, Pallas kernels for 0%

commit v1 on v0

--- a/solution.py
+++ b/solution.py
@@ -4,6 +4,12 @@
 from jax.sharding import PartitionSpec as P
 
 epsilon = 1e-05
+
+
+def gather_blocks(shard, mesh_axis, dim):
+    blocks = lax.all_gather(shard, mesh_axis, axis=0, tiled=False)
+    whole = jnp.concatenate(blocks, axis=dim)
+    return whole
 
 
 def layer_norm(values):
@@ -74,7 +80,7 @@
     column_panel = lax.all_gather(right_tile, "row", axis=0, tiled=True)
     triangle_in = jnp.einsum(
         "kih,kjh->ijh",
-        lax.all_gather(turned_left, "col", axis=1, tiled=True),
+        gather_blocks(turned_left, "col", 1),
         column_panel,
         preferred_element_type=jnp.float32,
     )

time: 163 us -> 164 us (level)
  local copies, waits for them, and re-layouts: 14 us -> 16.6 us
  waiting for transfers between devices: 59 us -> 57.3 us
    reshape x0 -> x1, local copies, waits for them, and re-layouts: none -> 2.93 us  [gather_blocks(): whole = jnp.concatenate(blocks, axis=dim)]
    all_gather x1, waiting for transfers between devices: 27.7 us -> 25.8 us  [gather_blocks(): blocks = lax.all_gather(shard, mesh_axis, axis=0, tiled=False)]
where the time goes in v1:
time: 164 us; the launch traced here: 163 us
  waiting for transfers between devices  57.3 us (35%)
  blocking collectives  53.1 us (32%)
  local copies, waits for them, and re-layouts  16.6 us (10%)
  matrix products  13.4 us (8%)
  between operations  13.4 us (8%)
  other arithmetic  8.93 us (5%)
    all_gather x1, waiting for transfers between devices, gather_blocks(): blocks = lax.all_gather(shard, mesh_axis, axis=0, tiled=False)  25.8 us
    all_gather x1, waiting for transfers between devices, shards(): lax.all_gather(turned_right, 'row', axis=0, tiled=True)  24.4 us
    all_to_all x1, blocking collectives, shards(): lax.all_to_all(lax.all_to_all(outbound, 'row', split_axis=0, concat_axis=...  21 us
    all_to_all x1, blocking collectives, shards(): lax.all_to_all(outbound_left, 'col', split_axis=1, concat_axis=1, tiled=T...  13.1 us
    all_to_all x1, blocking collectives, shards(): lax.all_to_all(outbound, 'row', split_axis=0, concat_axis=0, tiled=True)  10.7 us
    all_to_all x1, blocking collectives, shards(): lax.all_to_all(lax.all_to_all(outbound_left, 'col', split_axis=1, concat_...  8.25 us
    convert_element_type x2, local copies, waits for them, and re-layouts, finish(): tri_norm = layer_norm(triangle).astype(jnp.bfloat16)  5.27 us
    all_gather x1, waiting for transfers between devices, shards(): column_panel = lax.all_gather(right_tile, 'row', axis=0, tiled=True)  3.65 us
  transfers between devices with their start and end apart: 4, of which 4 were waited for; matrix products, arithmetic and copies ran while one was open for 6% of the time, Pallas kernels for 0%

profile of v1, /device:TPU:0, one launch (start us, length us, event | category | flops | bytes accessed | tf_op | source)
XLA Modules:
  0.0 162.9 jit_solution(3213414092409150214)
XLA Ops:
  6.5 1.2 convert_reduce_fusion
  7.8 1.3 fusion.19
  9.1 1.4 fusion.46
  10.6 1.3 fusion.48
  13.0 10.7 %all_to_all.43 = bf16[32,32,128]{2,1,0:T(8,128)(2,1)S(1)} all-to-all(bf16[32,32,128]{2,1,0:T(8,128)(2,1)S(1)} %get-tuple-element.8), channel_id=1, replica_groups=mesh['row'=4,'col'=4,'crop'=2] {'row'}, dimensions={0} | all-to-all | bytes 524288 | tf_op jit(solution)/shard_map/all_to_all | solution.py:55
  23.7 21.0 %all_to_all.44 = bf16[32,32,128]{2,1,0:T(8,128)(2,1)S(1)} all-to-all(bf16[32,32,128]{2,1,0:T(8,128)(2,1)S(1)} %all_to_all.43), channel_id=1, replica_groups=mesh['row'=4,'col'=4,'crop'=2] {'col'}, dimensions={0} | all-to-all | bytes 524288 | tf_op jit(solution)/shard_map/all_to_all | solution.py:54
  46.5 3.4 %all-gather.7.cloned.1.call-done = bf16[32,128,128]{2,1,0:T(8,128)(2,1)} async-done(((bf16[32,32,128]{2,1,0:T(8,128)(2,1)}), bf16[32,128,128]{2,1,0:T(8,128)(2,1)}) %all-gather.7.cloned.1.call-update) | async-done | bytes 1048592 | tf_op jit(solution)/shard_map/all_gather | solution.py:62
  49.9 2.7 %copy.66 = bf16[32,128,128]{1,0,2:T(8,128)(2,1)} copy(bf16[32,128,128]{2,1,0:T(8,128)(2,1)} %all-gather.7.cloned.1.call-done) | data formatting | bytes 2097152 | tf_op jit(solution)/shard_map/all_gather | solution.py:62
  52.5 24.4 %all-gather.5.cloned.1.call-done = bf16[32,128,128]{1,0,2:T(8,128)(2,1)} async-done(((bf16[8,128,128]{1,0,2:T(8,128)(2,1)}), bf16[32,128,128]{1,0,2:T(8,128)(2,1)}) %all-gather.5.cloned.1.call-update) | async-done | bytes 1048592 | tf_op jit(solution)/shard_map/all_gather | solution.py:66
  76.9 2.2 %bitcast_reduce_fusion.1 = (f32[32,32]{0,1:T(8,128)S(1)}, f32[128,32,32]{2,1,0:T(8,128)S(1)}) fusion(bf16[32,128,128]{1,0,2:T(8,128)(2,1)} %all-gather.5.cloned.1.call-done, bf16[32,128,128]{1,0,2:T(8,128)(2,1)} %copy.66), kind=kOutput, calls=%fused_computation.5 | convolution fusion | flops 33684480 | bytes 2625536 | tf_op jit(solution)/shard_map/ikh,jkh->ijh/dot_general | solution.py:63
  79.8 1.3 multiply_convert_fusion.1
  81.1 2.7 %copy.71 = bf16[32,32,128]{2,1,0:T(8,128)(2,1)S(1)} copy(bf16[32,32,128]{0,1,2:T(8,128)(2,1)} %multiply_convert_fusion.1) | data formatting | bytes 524288 | tf_op jit(solution)/shard_map/convert_element_type | solution.py:32
  86.7 13.1 %all_to_all.45 = bf16[32,32,128]{2,0,1:T(8,128)(2,1)S(1)} all-to-all(bf16[32,32,128]{2,0,1:T(8,128)(2,1)S(1)} %copy.72), channel_id=1, replica_groups=mesh['row'=4,'col'=4,'crop'=2] {'col'}, dimensions={1} | all-to-all | bytes 524288 | tf_op jit(solution)/shard_map/all_to_all | solution.py:73
  99.8 8.2 %all_to_all.46 = bf16[32,32,128]{2,0,1:T(8,128)(2,1)S(1)} all-to-all(bf16[32,32,128]{2,0,1:T(8,128)(2,1)S(1)} %all_to_all.45), channel_id=1, replica_groups=mesh['row'=4,'col'=4,'crop'=2] {'row'}, dimensions={1} | all-to-all | bytes 524288 | tf_op jit(solution)/shard_map/all_to_all | solution.py:72
  108.9 1.1 fusion.3
  109.9 3.7 %all-gather.9.cloned.1.call-done = bf16[128,32,128]{2,1,0:T(8,128)(2,1)} async-done(((bf16[32,32,128]{2,1,0:T(8,128)(2,1)}), bf16[128,32,128]{2,1,0:T(8,128)(2,1)}) %all-gather.9.cloned.1.call-update) | async-done | bytes 1048592 | tf_op jit(solution)/shard_map/all_gather | solution.py:80
  113.6 3.2 %copy.76 = bf16[128,32,128]{0,1,2:T(8,128)(2,1)} copy(bf16[128,32,128]{2,1,0:T(8,128)(2,1)} %all-gather.9.cloned.1.call-done) | data formatting | bytes 2097152 | tf_op jit(solution)/shard_map/all_gather | solution.py:80
  116.8 25.8 %all-gather.11.cloned.1.call-done = bf16[4,128,8,128]{3,2,1,0:T(8,128)(2,1)} async-done(((bf16[1,128,8,128]{3,2,1,0:T(8,128)(2,1)}), bf16[4,128,8,128]{3,2,1,0:T(8,128)(2,1)}) %all-gather.11.cloned.1.call-update) | async-done | bytes 1048592 | tf_op jit(solution)/shard_map/all_gather | solution.py:10
  142.6 2.9 %copy.75 = bf16[128,4,8,128]{0,2,1,3:T(8,128)(2,1)} copy(bf16[128,4,8,128]{3,2,0,1:T(8,128)(2,1)} %bitcast.70) | data formatting | bytes 2097152 | tf_op jit(solution)/shard_map/reshape | solution.py:11
  145.5 2.2 %bitcast_reduce_fusion = (f32[32,32]{0,1:T(8,128)S(1)}, f32[128,32,32]{2,1,0:T(8,128)S(1)}) fusion(bf16[128,32,128]{0,1,2:T(8,128)(2,1)} %copy.76, bf16[128,4,8,128]{0,2,1,3:T(8,128)(2,1)} %copy.75), kind=kOutput, calls=%fused_computation.3 | convolution fusion | flops 33684480 | bytes 2625536 | tf_op jit(solution)/shard_map/kih,kjh->ijh/dot_general | solution.py:81
  148.4 1.3 multiply_convert_fusion
  149.7 2.6 %copy.81 = bf16[32,32,128]{2,1,0:T(8,128)(2,1)S(1)} copy(bf16[32,32,128]{0,1,2:T(8,128)(2,1)} %multiply_convert_fusion) | data formatting | bytes 524288 | tf_op jit(solution)/shard_map/convert_element_type | solution.py:32
  152.3 1.4 fusion.63
  155.0 1.4 fusion.13
  (63 shorter events, 9.0 us)
Async XLA Ops:
  6.5 147.6 %copy-start = (bf16[128,1024]{1,0:T(8,128)(2,1)S(1)}, bf16[128,1024]{1,0:T(8,128)(2,1)}, u32[]{:S(2)}) copy-start(bf16[128,1024]{1,0:T(8,128)(2,1)} %param.22) | copy-start | bytes 786436
  6.5 4.0 %copy-start.1 = (bf16[32,32,128]{2,1,0:T(8,128)(2,1)S(1)}, bf16[32,32,128]{2,1,0:T(8,128)(2,1)}, u32[]{:S(2)}) copy-start(bf16[32,32,128]{2,1,0:T(8,128)(2,1)} %param.12) | copy-start | bytes 786436
  6.5 5.3 %copy-start.6 = (s32[32,32]{1,0:T(8,128)S(1)}, s32[32,32]{1,0:T(8,128)}, u32[]{:S(2)}) copy-start(s32[32,32]{1,0:T(8,128)} %param.13) | copy-start | bytes 12292
  6.5 43.3 %all-gather.7.cloned.1.call-start = ((), (), s32[]{:S(2)}) async-start(), calls=%async_computation.5 | async-start | bytes 1310720 | tf_op jit(solution)/shard_map/all_gather | solution.py:62
  11.9 33.8 %copy-start.8 = (bf16[128,128]{1,0:T(8,128)(2,1)S(1)}, bf16[128,128]{1,0:T(8,128)(2,1)}, u32[]{:S(2)}) copy-start(bf16[128,128]{1,0:T(8,128)(2,1)} %param.16) | copy-start | bytes 98308
  12.9 64.0 %all-gather.5.cloned.1.call-start = ((), (), s32[]{:S(2)}) async-start(), calls=%async_computation.4 | async-start | bytes 1310720 | tf_op jit(solution)/shard_map/all_gather | solution.py:66
  45.7 67.9 %all-gather.9.cloned.1.call-start = ((), (), s32[]{:S(2)}) async-start(), calls=%async_computation.6 | async-start | bytes 1310720 | tf_op jit(solution)/shard_map/all_gather | solution.py:80
  79.8 3.9 %copy-start.5 = (bf16[128,128]{1,0:T(8,128)(2,1)S(1)}, bf16[128,128]{1,0:T(8,128)(2,1)}, u32[]{:S(2)}) copy-start(bf16[128,128]{1,0:T(8,128)(2,1)} %param.17) | copy-start | bytes 98308
  81.1 3.8 %copy-start.2 = (bf16[128,256]{1,0:T(8,128)(2,1)S(1)}, bf16[128,256]{1,0:T(8,128)(2,1)}, u32[]{:S(2)}) copy-start(bf16[128,256]{1,0:T(8,128)(2,1)} %param.18) | copy-start | bytes 196612
  83.7 1.4 copy-start.3
  85.5 23.4 %copy-start.9 = (bf16[128,128]{1,0:T(8,128)(2,1)S(1)}, bf16[128,128]{1,0:T(8,128)(2,1)}, u32[]{:S(2)}) copy-start(bf16[128,128]{1,0:T(8,128)(2,1)} %param.20) | copy-start | bytes 98308
  86.5 56.1 %all-gather.11.cloned.1.call-start = ((), (), s32[]{:S(2)}) async-start(), calls=%async_computation.7 | async-start | bytes 1310720 | tf_op jit(solution)/shard_map/all_gather | solution.py:10
  148.4 3.9 %copy-start.4 = (bf16[128,128]{1,0:T(8,128)(2,1)S(1)}, bf16[128,128]{1,0:T(8,128)(2,1)}, u32[]{:S(2)}) copy-start(bf16[128,128]{1,0:T(8,128)(2,1)} %param.21) | copy-start | bytes 98308
  154.1 0.9 copy-start.7
Sparse Core Ops, SparseCore 0:
  13.1 36.7 all-gather.6
  51.7 25.2 all-gather.4
  86.6 26.9 all-gather.8
  115.0 27.5 all-gather.10
